TPU v7x, 128 devices: a whole 4x4x4 slice. The times are simulated.
128 devices in a mesh: data: 1, model: 2 (over core), seq: 64 (over z, y, x).
Axes of the slice: x: 4, y: 4, z: 4, core: 2. Of those that a mesh axis runs over, the one named last changes fastest.
Arguments:
- hidden: bfloat16 [64, 3584], P(('data', 'seq'))
- k_cache: bfloat16 [64, 8192, 4, 128], P('data', 'seq', 'model')
- v_cache: bfloat16 [64, 8192, 4, 128], P('data', 'seq', 'model')
- sel_blocks: int32 [64, 4, 32], P('data')
- g_attn: bfloat16 [3584], replicated
- g_mlp: bfloat16 [3584], replicated
- w_q: bfloat16 [3584, 3584], replicated
- w_o: bfloat16 [3584, 3584], replicated
- w_gate: bfloat16 [3584, 18944], P(None, 'model')
- w_up: bfloat16 [3584, 18944], P(None, 'model')
- w_down: bfloat16 [18944, 3584], P('model')
Outputs:
- output: bfloat16 [64, 3584], P(('data', 'seq'))
All inputs are finite; a program needn't handle non-finite values.
Results may differ from a plain program's by a relative error of at most 0.0123724.
Values are sent between devices in bfloat16 or wider.
A program may use at most 1 GiB of HBM per device.

v0:
```python
import jax
import jax.numpy as jnp
from jax import lax
from jax.sharding import PartitionSpec as P

BLOCK_LEN = 64
NORM_EPS = 1e-5


def rms_norm(hidden, gain_vec):
    hid_f32 = hidden.astype(jnp.float32)
    inv_rms = lax.rsqrt(jnp.mean(hid_f32 * hid_f32, axis=-1, keepdims=True) + NORM_EPS)
    return (hid_f32 * inv_rms * gain_vec.astype(jnp.float32)).astype(jnp.bfloat16)


def block_cap(top_blocks, seq_devs):
    return min(top_blocks - 1, max(2, (2 * top_blocks + seq_devs - 1) // seq_devs))


def solution(mesh):
    model_devs = mesh.shape["model"]
    seq_devs = mesh.shape["seq"]
    pick_blocks = jax.vmap(jax.vmap(lambda cache_h, idx_h: cache_h[idx_h], in_axes=(2, 0)))

    def device_step(hidden, k_cache, v_cache, sel_blocks, g_attn, g_mlp, w_q, w_o, w_gate, w_up, w_down):
        home_rows = hidden.shape[0]
        batch_size, tokens_dev, kv_local, head_dim = k_cache.shape
        top_blocks = sel_blocks.shape[2]
        heads_local = w_q.shape[1] // (head_dim * model_devs)
        group_size = heads_local // kv_local
        width_local = heads_local * head_dim
        blocks_dev = tokens_dev // BLOCK_LEN
        slot_cap = block_cap(top_blocks, seq_devs)
        model_idx = lax.axis_index("model")
        seq_idx = lax.axis_index("seq")

        h_attn = rms_norm(hidden, g_attn)
        wq_local = lax.dynamic_slice_in_dim(w_q, model_idx * width_local, width_local, axis=1)
        queries = (jnp.dot(h_attn, wq_local, preferred_element_type=jnp.float32) * head_dim ** -0.5).astype(jnp.bfloat16)
        queries = queries.reshape(home_rows, kv_local, group_size, head_dim)

        sel_local = lax.dynamic_slice_in_dim(sel_blocks, model_idx * kv_local, kv_local, axis=1)
        owner_dev = sel_local // blocks_dev
        is_mine = (owner_dev == seq_idx).astype(jnp.int32)
        rank_mine = jnp.cumsum(is_mine, axis=-1) - 1
        slot_ids = jnp.arange(slot_cap, dtype=jnp.int32)
        slot_hit = (is_mine[..., None] == 1) & (rank_mine[..., None] == slot_ids)
        local_ids = jnp.sum(jnp.where(slot_hit, (sel_local % blocks_dev)[..., None], 0), axis=2)
        block_shape = (batch_size, blocks_dev, BLOCK_LEN, kv_local, head_dim)
        send_shape = (seq_devs, home_rows, kv_local, slot_cap, BLOCK_LEN, head_dim)
        k_send = pick_blocks(k_cache.reshape(block_shape), local_ids).reshape(send_shape)
        v_send = pick_blocks(v_cache.reshape(block_shape), local_ids).reshape(send_shape)
        k_recv = lax.all_to_all(k_send, "seq", 0, 0, tiled=True)
        v_recv = lax.all_to_all(v_send, "seq", 0, 0, tiled=True)

        sel_home = lax.dynamic_slice_in_dim(sel_local, seq_idx * home_rows, home_rows, axis=0)
        holder_ids = jnp.arange(seq_devs, dtype=jnp.int32)
        held_count = jnp.sum((sel_home[..., None] // blocks_dev == holder_ids).astype(jnp.int32), axis=2)
        slot_valid = slot_ids < held_count[..., None]
        scores = jnp.einsum("bgrd,sbgctd->bgrsct", queries, k_recv, preferred_element_type=jnp.float32)
        scores = jnp.where(slot_valid[:, :, None, :, :, None], scores, -jnp.inf)
        top_score = jnp.max(scores, axis=(3, 4, 5), keepdims=True)
        weights = jnp.exp(scores - top_score)
        exp_sum = jnp.sum(weights, axis=(3, 4, 5))
        weighted = jnp.einsum("bgrsct,sbgctd->bgrd", weights.astype(jnp.bfloat16), v_recv, preferred_element_type=jnp.float32)
        attn_out = (weighted / exp_sum[..., None]).astype(jnp.bfloat16).reshape(home_rows, width_local)

        wo_local = lax.dynamic_slice_in_dim(w_o, model_idx * width_local, width_local, axis=0)
        attn_proj = lax.psum(jnp.dot(attn_out, wo_local, preferred_element_type=jnp.float32), "model")
        resid_mid = (hidden.astype(jnp.float32) + attn_proj).astype(jnp.bfloat16)
        h_mlp = rms_norm(resid_mid, g_mlp)
        gate_act = jnp.dot(h_mlp, w_gate, preferred_element_type=jnp.float32).astype(jnp.bfloat16)
        up_act = jnp.dot(h_mlp, w_up, preferred_element_type=jnp.float32).astype(jnp.bfloat16)
        hidden_act = (jax.nn.silu(gate_act.astype(jnp.float32)) * up_act.astype(jnp.float32)).astype(jnp.bfloat16)
        mlp_out = lax.psum(jnp.dot(hidden_act, w_down, preferred_element_type=jnp.float32), "model")
        return (resid_mid.astype(jnp.float32) + mlp_out).astype(jnp.bfloat16)

    cache_spec = P("data", "seq", "model", None)
    in_specs = (P(("data", "seq"), None), cache_spec, cache_spec, P("data", None, None), P(None), P(None), P(None, None), P(None, None), P(None, "model"), P(None, "model"), P("model", None))
    return jax.shard_map(device_step, mesh=mesh, in_specs=in_specs, out_specs=P(("data", "seq"), None), check_vma=False)
```

profile of v0, /device:TPU:1, one launch (start us, length us, event | category | flops | bytes accessed | tf_op | source)
XLA Modules:
  0.0 245.2 jit_solution(3307371775827318749)
XLA Ops:
  0.0 0.0 copy-start
  0.0 0.8 copy-done
  0.8 0.1 copy.51
  1.0 0.1 broadcast_compare_fusion
  1.0 0.4 reduce_window_sum.11
  1.5 0.1 copy.41
  1.5 0.1 copy.40
  1.6 0.1 copy.42
  1.8 0.1 copy.43
  1.9 0.2 reshape.217
  2.0 5.3 %copy.38 = bf16[64,128,2,128]{3,1,2,0:T(8,128)(2,1)} copy(bf16[64,128,2,128]{3,2,1,0:T(2,128)(2,1)} %param.12) | data formatting | bytes 8388608 | tf_op args[1]
  7.3 5.8 %gather_fusion = bf16[256,64,128]{2,1,0:T(8,128)(2,1)} fusion(bf16[64,2,2,64,128]{4,3,2,1,0:T(8,128)(2,1)} %bitcast.61, s32[256]{0:T(256)S(1)} %reshape.217), kind=kCustom, calls=%fused_computation | custom fusion | bytes 8391680 | tf_op jit(solution)/shard_map/vmap(vmap())/gather | solution.py:23
  13.1 12.2 %all-to-all-start = ((bf16[64,1,2,2,64,128]{5,4,3,2,1,0:T(8,128)(2,1)}), bf16[64,1,2,2,64,128]{5,4,3,2,1,0:T(8,128)(2,1)}, u32[]{:S(2)}, u32[]{:S(2)}) async-start(bf16[64,1,2,2,64,128]{5,4,3,2,1,0:T(8,128)(2,1)} %bitcast.59), calls=%async_computation | async-start | bytes 8388608 | tf_op jit(solution)/shard_map/all_to_all | solution.py:53
  25.3 5.3 %copy.46 = bf16[64,128,2,128]{3,1,2,0:T(8,128)(2,1)} copy(bf16[64,128,2,128]{3,2,1,0:T(2,128)(2,1)} %param.13) | data formatting | bytes 8388608 | tf_op args[2]
  30.6 5.8 %gather_fusion.1 = bf16[256,64,128]{2,1,0:T(8,128)(2,1)} fusion(bf16[64,2,2,64,128]{4,3,2,1,0:T(8,128)(2,1)} %bitcast.60, s32[256]{0:T(256)S(1)} %reshape.217), kind=kCustom, calls=%fused_computation.1 | custom fusion | bytes 8391680 | tf_op jit(solution)/shard_map/vmap(vmap())/gather | solution.py:23
  36.4 50.0 %all-to-all-done = bf16[64,1,2,2,64,128]{5,4,3,2,1,0:T(8,128)(2,1)} async-done(((bf16[64,1,2,2,64,128]{5,4,3,2,1,0:T(8,128)(2,1)}), bf16[64,1,2,2,64,128]{5,4,3,2,1,0:T(8,128)(2,1)}, u32[]{:S(2)}, u32[]{:S(2)}) %all-to-all-start) | async-done | bytes 4194336 | tf_op jit(solution)/shard_map/all_to_all | solution.py:53
  86.4 0.0 copy-start.3
  86.4 0.0 copy-start.2
  86.4 9.3 %all-to-all-start.1 = ((bf16[64,1,2,2,64,128]{5,4,3,2,1,0:T(8,128)(2,1)}), bf16[64,1,2,2,64,128]{5,4,3,2,1,0:T(8,128)(2,1)}, u32[]{:S(2)}, u32[]{:S(2)}) async-start(bf16[64,1,2,2,64,128]{5,4,3,2,1,0:T(8,128)(2,1)} %bitcast.58), calls=%async_computation.1 | async-start | bytes 8388608 | tf_op jit(solution)/shard_map/all_to_all | solution.py:54
  95.7 0.0 copy-done.3
  95.8 0.0 copy-done.2
  95.8 0.6 multiply_reduce_fusion.1
  97.1 0.0 copy-start.4
  97.1 6.4 %fusion.21 = f32[1792]{0:T(1024)S(1)} fusion(bf16[3584,3584]{1,0:T(8,128)(2,1)} %param.17, s32[]{:T(128)S(6)} %select_n.61, f32[3584]{0:T(1024)S(1)} %broadcast_in_dim.62, bf16[1,3584]{1,0:T(2,128)(2,1)S(1)} %copy-done.2, f32[]{:T(128)S(6)} %rsqrt.8), kind=kOutput, calls=%fused_computation.17 | convolution fusion | flops 12859392 | bytes 12873736 | tf_op jit(solution)/shard_map/dot_general | solution.py:39
  103.6 0.0 copy-done.4
  103.6 0.2 dynamic-slice_reduce_fusion
  103.8 0.1 convert_reduce_fusion
  103.9 0.1 iota_compare_fusion.1
  104.0 5.2 %fusion.55 = (f32[2,7]{1,0:T(2,128)S(1)}, f32[2,7,64,2,64]{4,1,3,2,0:T(8,128)S(1)}) fusion(bf16[64,1,2,2,64,128]{5,4,3,2,1,0:T(8,128)(2,1)} %all-to-all-done, bf16[2,7,128,1,1]{2,1,0,3,4:T(8,128)(2,1)S(1)} %reshape.233, pred[2,64,2]{2,1,0:T(8,128)(4,1)S(1)} %iota_compare_fusion.1), kind=kOutput, calls=%fused_computation.75 | convolution fusion | flops 29589490 | bytes 4656952 | tf_op jit(solution)/shard_map/bgrd,sbgctd->bgrsct/dot_general | solution.py:60
  109.2 0.4 fusion.24
  109.6 43.3 %all-to-all-done.1 = bf16[64,1,2,2,64,128]{5,4,3,2,1,0:T(8,128)(2,1)} async-done(((bf16[64,1,2,2,64,128]{5,4,3,2,1,0:T(8,128)(2,1)}), bf16[64,1,2,2,64,128]{5,4,3,2,1,0:T(8,128)(2,1)}, u32[]{:S(2)}, u32[]{:S(2)}) %all-to-all-start.1) | async-done | bytes 4194336 | tf_op jit(solution)/shard_map/all_to_all | solution.py:54
  153.0 2.9 %fusion.18 = bf16[2,7,128]{2,1,0:T(8,128)(2,1)S(1)} fusion(bf16[64,1,2,2,64,128]{5,4,3,2,1,0:T(8,128)(2,1)} %all-to-all-done.1, bf16[2,7,64,2,64]{4,1,3,2,0:T(8,128)(2,1)S(1)} %get-tuple-element.10, f32[2,7]{1,0:T(2,128)S(1)} %get-tuple-element.9), kind=kOutput, calls=%fused_computation.16 | convolution fusion | flops 29363712 | bytes 4427320 | tf_op jit(solution)/shard_map/bgrsct,sbgctd->bgrd/dot_general | solution.py:65
  156.0 6.4 %fusion = f32[1,3584]{1,0:T(1,128)S(1)} fusion(bf16[1792,1]{0,1:T(2,128)(2,1)S(1)} %reshape.235, bf16[3584,3584]{1,0:T(8,128)(2,1)} %param.18, s32[]{:T(128)S(6)} %select_n.61), kind=kOutput, calls=%fused_computation.2 | convolution fusion | flops 12845056 | bytes 12862980 | tf_op jit(solution)/shard_map/dot_general | solution.py:69
  162.4 7.8 %psum.14 = f32[1,3584]{1,0:T(1,128)S(1)} all-reduce(f32[1,3584]{1,0:T(1,128)S(1)} %fusion), channel_id=1, replica_groups=mesh['data'=1,'model'=2,'seq'=64] {'model'}, use_global_device_ids=true, to_apply=%region_6.7 | all-reduce | flops 3584 | bytes 28672 | tf_op jit(solution)/shard_map/psum | solution.py:69
  170.2 0.6 multiply_reduce_fusion
  171.5 23.0 %convolution_reduce_fusion.1 = bf16[9472]{0:T(1024)(128)(2,1)S(1)} fusion(bf16[3584,9472]{1,0:T(8,128)(2,1)} %param.19, f32[3584]{0:T(1024)S(1)} %broadcast_in_dim.63, bf16[1,3584]{1,0:T(2,128)(2,1)S(1)} %get-tuple-element.6, f32[]{:T(128)S(6)} %rsqrt.9), kind=kOutput, calls=%fused_computation.13 | convolution fusion | flops 67909632 | bytes 67935744 | tf_op jit(solution)/shard_map/dot_general | solution.py:72
  194.5 23.0 %convolution_reduce_fusion = bf16[9472]{0:T(1024)(128)(2,1)S(1)} fusion(bf16[3584,9472]{1,0:T(8,128)(2,1)} %param.20, f32[3584]{0:T(1024)S(1)} %broadcast_in_dim.63, bf16[1,3584]{1,0:T(2,128)(2,1)S(1)} %get-tuple-element.6, f32[]{:T(128)S(6)} %rsqrt.9), kind=kOutput, calls=%fused_computation.12 | convolution fusion | flops 67909632 | bytes 67935744 | tf_op jit(solution)/shard_map/dot_general | solution.py:73
  217.6 0.0 copy-start.1
  217.6 23.7 %fusion.56 = f32[1,3584]{1,0:T(1,128)S(1)} fusion(bf16[9472,1]{0,1:T(2,128)(2,1)S(1)} %reshape.241, bf16[9472,3584]{1,0:T(8,128)(2,1)} %param.21), kind=kOutput, calls=%fused_computation.76 | convolution fusion | flops 67895296 | bytes 67928576 | tf_op jit(solution)/shard_map/dot_general | solution.py:75
  241.3 3.3 %psum.15 = f32[1,3584]{1,0:T(1,128)S(1)} all-reduce(f32[1,3584]{1,0:T(1,128)S(1)} %fusion.56), channel_id=1, replica_groups=mesh['data'=1,'model'=2,'seq'=64] {'model'}, use_global_device_ids=true, to_apply=%region_8.9 | all-reduce | flops 3584 | bytes 28672 | tf_op jit(solution)/shard_map/psum | solution.py:75
  244.6 0.6 add_convert_fusion
  245.2 0.0 copy-done.1
  (13 shorter events, 0.2 us)
Async XLA Ops:
  0.0 0.8 copy-start
  13.1 73.3 %all-to-all-start = ((bf16[64,1,2,2,64,128]{5,4,3,2,1,0:T(8,128)(2,1)}), bf16[64,1,2,2,64,128]{5,4,3,2,1,0:T(8,128)(2,1)}, u32[]{:S(2)}, u32[]{:S(2)}) async-start(bf16[64,1,2,2,64,128]{5,4,3,2,1,0:T(8,128)(2,1)} %bitcast.59), calls=%async_computation | async-start | bytes 8388608 | tf_op jit(solution)/shard_map/all_to_all | solution.py:53
  86.4 9.3 %copy-start.3 = (bf16[3584]{0:T(1024)(128)(2,1)S(1)}, bf16[3584]{0:T(1024)(128)(2,1)}, u32[]{:S(2)}) copy-start(bf16[3584]{0:T(1024)(128)(2,1)} %param.15) | copy-start | bytes 21508
  86.4 9.3 %copy-start.2 = (bf16[1,3584]{1,0:T(2,128)(2,1)S(1)}, bf16[1,3584]{1,0:T(2,128)(2,1)}, u32[]{:S(2)}) copy-start(bf16[1,3584]{1,0:T(2,128)(2,1)} %param.11) | copy-start | bytes 21508
  86.4 66.6 %all-to-all-start.1 = ((bf16[64,1,2,2,64,128]{5,4,3,2,1,0:T(8,128)(2,1)}), bf16[64,1,2,2,64,128]{5,4,3,2,1,0:T(8,128)(2,1)}, u32[]{:S(2)}, u32[]{:S(2)}) async-start(bf16[64,1,2,2,64,128]{5,4,3,2,1,0:T(8,128)(2,1)} %bitcast.58), calls=%async_computation.1 | async-start | bytes 8388608 | tf_op jit(solution)/shard_map/all_to_all | solution.py:54
  97.1 6.5 %copy-start.4 = (bf16[3584]{0:T(1024)(128)(2,1)S(1)}, bf16[3584]{0:T(1024)(128)(2,1)}, u32[]{:S(2)}) copy-start(bf16[3584]{0:T(1024)(128)(2,1)} %param.16) | copy-start | bytes 21508
  217.6 27.6 %copy-start.1 = (s32[64,4,32]{0,2,1:T(8,128)S(1)}, s32[64,4,32]{0,2,1:T(8,128)}, u32[]{:S(2)}) copy-start(s32[64,4,32]{0,2,1:T(8,128)} %param.14) | copy-start | bytes 98308
where the time goes:
time: 246 us; the launch traced here: 245 us
  waiting for transfers between devices  93.3 us (38%)
  matrix products  90.7 us (37%)
  local copies, waits for them, and re-layouts  23.8 us (10%)
  starting transfers between devices  21.5 us (9%)
  blocking collectives  11.2 us (5%)
  other arithmetic  3.1 us (1%)
    all_to_all x1, waiting for transfers between devices, device_step(): k_recv = lax.all_to_all(k_send, 'seq', 0, 0, tiled=True)  50 us
    all_to_all x1, waiting for transfers between devices, device_step(): v_recv = lax.all_to_all(v_send, 'seq', 0, 0, tiled=True)  43.3 us
    dot_general x1, matrix products, device_step(): jnp.dot(hidden_act, w_down, preferred_element_type=jnp.float32)  23.7 us
    dot_general x1, matrix products, device_step(): jnp.dot(h_mlp, w_up, preferred_element_type=jnp.float32)  23 us
    dot_general x1, matrix products, device_step(): jnp.dot(h_mlp, w_gate, preferred_element_type=jnp.float32)  23 us
    all_to_all x1, starting transfers between devices, device_step(): k_recv = lax.all_to_all(k_send, 'seq', 0, 0, tiled=True)  12.2 us
    gather x4, local copies, waits for them, and re-layouts, solution(): cache_h[idx_h]  11.8 us
    unnamed x13, local copies, waits for them, and re-layouts  11.5 us
  transfers between devices with their start and end apart: 2, of which 2 were waited for; matrix products, arithmetic and copies ran while one was open for 10% of the time, Pallas kernels for 0%

commit v1 on v0

v1 whole, which is shorter than its diff:
```python
import functools

import jax
import jax.numpy as jnp
from jax import lax
from jax.experimental import pallas as pl
from jax.experimental.pallas import tpu as pltpu
from jax.sharding import PartitionSpec as P

MESH = pl.DeviceIdType.MESH
BLOCK_LEN = 64
NORM_EPS = 1e-5
LANES = 128
NEG_INF = float("-inf")
F32 = jnp.float32
BF16 = jnp.bfloat16


def row_iota(shape):
    return lax.broadcasted_iota(jnp.int32, shape, 0)


def decode_kernel(
    cfg,
    small_ref, sel_ref, k_hbm, v_hbm, wq_hbm, wo_hbm, wg_hbm, wu_hbm, wd_hbm,
    out_ref,
    k_buf, v_buf, wq_buf, wo_buf, wg_buf, wu_buf, wd_buf,
    hit_buf, lhs_buf, olhs_buf, q_all, part_out, part_in, stat_buf,
    pair_out, pair_in, h2_all, mlp_out, mlp_in, fin_out, fin_in,
    wq_sem, kv_sem, wo_sem, mlp_sem,
    q_send, q_recv, part_send, part_recv, pair_send, pair_recv, h2_send, h2_recv,
    red_send, red_recv, fin_send, fin_recv,
):
    seqs, plane, n_md, tiles_ffn, tiles_max = cfg
    planes = seqs // plane
    core = lax.axis_index("model")
    me = lax.axis_index("seq")
    my_plane = me // plane
    my_slot = me % plane
    heads = 14
    width = heads * LANES
    q_chunks = wq_buf.shape[0]
    o_chunks = wo_buf.shape[0]
    model_dim = n_md * LANES
    pad_md = small_ref.shape[1]

    def wq_copy(n):
        cols = pl.ds(pl.multiple_of(core * width + n * 256, LANES), 256)
        return pltpu.make_async_copy(wq_hbm.at[:, cols], wq_buf.at[n], wq_sem.at[n])

    def kv_copy(which, zz):
        src, dst = ((k_hbm, k_buf), (v_hbm, v_buf))[which]
        rows = pl.ds(zz * plane, plane)
        return pltpu.make_async_copy(src.at[rows], dst.at[rows], kv_sem.at[which, zz])

    def wo_copy(n):
        rows = pl.ds(pl.multiple_of(core * width, LANES), width)
        return pltpu.make_async_copy(wo_hbm.at[rows, pl.ds(n * 512, 512)], wo_buf.at[n], wo_sem.at[n])

    first_tile = (tiles_ffn * my_slot) // plane
    my_tiles = (tiles_ffn * (my_slot + 1)) // plane - first_tile
    ffn_cols = pl.ds(pl.multiple_of(first_tile * LANES, LANES), tiles_max * LANES)
    wg_copy = pltpu.make_async_copy(wg_hbm.at[:, ffn_cols], wg_buf, mlp_sem.at[0])
    wu_copy = pltpu.make_async_copy(wu_hbm.at[:, ffn_cols], wu_buf, mlp_sem.at[1])
    wd_copy = pltpu.make_async_copy(wd_hbm.at[ffn_cols, :], wd_buf, mlp_sem.at[2])

    for n in range(q_chunks):
        wq_copy(n).start()

    barrier = pltpu.get_barrier_semaphore()

    @pl.loop(1, seqs)
    def _(d):
        pl.semaphore_signal(barrier, inc=1, device_id={"seq": lax.rem(me + d, seqs)}, device_id_type=MESH)

    pl.semaphore_signal(barrier, inc=1, device_id={"model": 1 - core}, device_id_type=MESH)

    rows8 = row_iota((8, LANES))
    rows16 = row_iota((16, LANES))
    lane16 = lax.broadcasted_iota(jnp.int32, (16, LANES), 1)
    hid = small_ref[0].astype(F32)
    gain_attn = small_ref[1].astype(F32)
    gain_mlp = small_ref[2].astype(F32)

    def norm(x, gain):
        inv = lax.rsqrt(jnp.sum(x * x, keepdims=True) / model_dim + NORM_EPS)
        return (x * inv * gain).astype(BF16)

    h_attn = norm(hid, gain_attn).astype(F32)
    for n in range(n_md):
        lhs_buf[:, n * LANES:(n + 1) * LANES] = jnp.broadcast_to(h_attn[n:n + 1, :], (16, LANES)).astype(BF16)

    for j in range(2):
        block_id = me * 2 + j

        @pl.loop(0, seqs // 8)
        def _(b):
            sel = sel_ref[pl.ds(b * 8, 8)]
            found = jnp.max(jnp.where(sel == block_id, 1.0, 0.0), axis=2, keepdims=True)
            hit_buf[j, pl.ds(b * 8, 8)] = jnp.broadcast_to(jnp.where(found > 0.5, 0.0, NEG_INF), (8, 4, LANES))

    q_tile = jnp.zeros((16, LANES), F32)
    for n in range(q_chunks):
        wq_copy(n).wait()
        acc = jnp.dot(lhs_buf[...], wq_buf[n], preferred_element_type=F32) * (LANES ** -0.5)
        q_tile = jnp.where(rows16 == 2 * n, acc[:, :LANES], q_tile)
        q_tile = jnp.where(rows16 == 2 * n + 1, acc[:, LANES:], q_tile)
    q_all[me] = q_tile.astype(BF16)

    plane_order = [0, 1, planes - 1] + list(range(2, planes - 1)) if planes > 2 else list(range(planes))
    plane_ids = [lax.rem(my_plane + k, planes) for k in plane_order]
    for zz in plane_ids:
        kv_copy(0, zz).start()
        kv_copy(1, zz).start()
    for n in range(o_chunks):
        wo_copy(n).start()
    wg_copy.start()
    wu_copy.start()
    wd_copy.start()

    pl.semaphore_wait(barrier, seqs)

    def q_push(to):
        return pltpu.make_async_remote_copy(
            src_ref=q_all.at[me], dst_ref=q_all.at[me], send_sem=q_send, recv_sem=q_recv.at[my_plane],
            device_id={"seq": to}, device_id_type=MESH)

    @pl.loop(1, plane)
    def _(d):
        q_push(my_plane * plane + lax.rem(my_slot + d, plane)).start()

    for zz in plane_ids[1:]:
        @pl.loop(0, plane)
        def _(d):
            q_push(zz * plane + lax.rem(my_slot + d, plane)).start()

    parity = ((lane16 % 2) == jnp.where(rows16 < 7, 0, 1)) & (rows16 < heads)

    def part_push(to):
        return pltpu.make_async_remote_copy(
            src_ref=part_out.at[to], dst_ref=part_in.at[me], send_sem=part_send, recv_sem=part_recv,
            device_id={"seq": to}, device_id_type=MESH)

    for k, zz in enumerate(plane_ids):
        base = zz * plane
        if k == 0:
            if plane > 1:
                gone = q_all.at[pl.ds(0, plane - 1)]
                pltpu.make_async_copy(gone, gone, q_recv.at[zz]).wait()
        else:
            whole = q_all.at[pl.ds(0, plane)]
            pltpu.make_async_copy(whole, whole, q_recv.at[zz]).wait()
        kv_copy(0, zz).wait()
        kv_copy(1, zz).wait()
        stats = jnp.zeros((16, LANES), F32)
        for i in range(plane):
            row = base + i
            scores = lax.dot_general(q_all[row], k_buf[row], (((1,), (1,)), ((), ())), preferred_element_type=F32)
            masked = []
            for j in range(2):
                hit_0 = jnp.broadcast_to(hit_buf[j, row, pl.ds(2 * core, 1), :], (16, LANES))
                hit_1 = jnp.broadcast_to(hit_buf[j, row, pl.ds(2 * core + 1, 1), :], (16, LANES))
                bias = jnp.where(parity, jnp.where(rows16 < 7, hit_0, hit_1), NEG_INF)
                masked.append(scores[:, j * LANES:(j + 1) * LANES] + bias)
            top = jnp.max(jnp.maximum(masked[0], masked[1]), axis=1, keepdims=True)
            safe = jnp.where(top == NEG_INF, 0.0, top)
            exps = [jnp.exp(s - safe) for s in masked]
            total = jnp.sum(exps[0] + exps[1], axis=1, keepdims=True)
            weights = jnp.concatenate([e.astype(BF16) for e in exps], axis=1)
            part_out[row] = jnp.dot(weights, v_buf[row], preferred_element_type=F32)
            stats = jnp.where(lane16 == i, top, stats)
            stats = jnp.where(lane16 == plane + i, total, stats)
        stats_t = stats.T
        for i in range(plane):
            row = base + i
            part_out[row, 14:15, 0:16] = stats_t[i:i + 1, :]
            part_out[row, 15:16, 0:16] = stats_t[plane + i:plane + i + 1, :]
        for i in range(plane):
            if k == 0:
                @pl.when(i != my_slot)
                def _():
                    part_push(base + i).start()
            else:
                part_push(base + i).start()

    part_in[me] = part_out[me]
    others = part_in.at[pl.ds(0, seqs - 1)]
    pltpu.make_async_copy(others, others, part_recv).wait()
    for i in range(seqs):
        stat_buf[i:i + 1, :] = part_in[i, 14:15, :]
    head_lane = lax.broadcasted_iota(jnp.int32, (seqs, LANES), 1) < heads
    tops = jnp.where(head_lane, stat_buf[0:seqs, :], 0.0)
    scale = jnp.exp(tops - jnp.max(tops, axis=0, keepdims=True))
    for i in range(seqs):
        stat_buf[i:i + 1, :] = part_in[i, 15:16, :]
    sums = jnp.where(head_lane, stat_buf[0:seqs, :], 0.0)
    denom = jnp.sum(scale * sums, axis=0, keepdims=True)
    stat_buf[0:seqs, :] = scale
    stat_buf[seqs:seqs + 8, :] = jnp.broadcast_to(denom, (8, LANES))
    scale_t = stat_buf[...].T
    acc = jnp.zeros((16, LANES), F32)
    for i in range(seqs):
        acc = acc + scale_t[0:16, i:i + 1] * part_in[i]
    attn = (acc / jnp.where(rows16 < heads, scale_t[0:16, seqs:seqs + 1], 1.0)).astype(BF16).astype(F32)
    for r in range(heads):
        olhs_buf[:, r * LANES:(r + 1) * LANES] = jnp.broadcast_to(attn[r:r + 1, :], (16, LANES)).astype(BF16)

    proj = [jnp.zeros((8, LANES), F32) for _ in range(pad_md // 8)]
    for n in range(o_chunks):
        wo_copy(n).wait()
        acc = jnp.dot(olhs_buf[...], wo_buf[n], preferred_element_type=F32)
        for t in range(4):
            r = 4 * n + t
            proj[r // 8] = jnp.where(rows8 == r % 8, acc[0:8, t * LANES:(t + 1) * LANES], proj[r // 8])
    for r in range(pad_md // 8):
        pair_out[r * 8:(r + 1) * 8, :] = proj[r]
    pair = pltpu.make_async_remote_copy(
        src_ref=pair_out, dst_ref=pair_in, send_sem=pair_send, recv_sem=pair_recv,
        device_id={"model": 1 - core}, device_id_type=MESH)
    pair.start()
    pair.wait()
    resid = (hid + (pair_out[...] + pair_in[...])).astype(BF16).astype(F32)
    h2_all[my_slot] = norm(resid, gain_mlp)

    def h2_push(to_slot):
        return pltpu.make_async_remote_copy(
            src_ref=h2_all.at[my_slot], dst_ref=h2_all.at[my_slot], send_sem=h2_send, recv_sem=h2_recv,
            device_id={"seq": my_plane * plane + to_slot}, device_id_type=MESH)

    @pl.loop(1, plane)
    def _(d):
        h2_push(lax.rem(my_slot + d, plane)).start()

    gone = h2_all.at[pl.ds(0, plane - 1)]
    pltpu.make_async_copy(gone, gone, h2_recv).wait()
    rows = [h2_all[i].astype(F32) for i in range(plane)]
    for n in range(n_md):
        tile = jnp.zeros((16, LANES), F32)
        for i in range(plane):
            tile = jnp.where(rows16 == i, jnp.broadcast_to(rows[i][n:n + 1, :], (16, LANES)), tile)
        lhs_buf[:, n * LANES:(n + 1) * LANES] = tile.astype(BF16)

    wg_copy.wait()
    gate = jnp.dot(lhs_buf[...], wg_buf[...], preferred_element_type=F32).astype(BF16).astype(F32)
    wu_copy.wait()
    up = jnp.dot(lhs_buf[...], wu_buf[...], preferred_element_type=F32).astype(BF16).astype(F32)
    act = jax.nn.silu(gate) * up
    cols = lax.broadcasted_iota(jnp.int32, act.shape, 1)
    act = jnp.where(cols < my_tiles * LANES, act, 0.0).astype(BF16)
    wd_copy.wait()
    for n in range(o_chunks):
        acc = jnp.dot(act, wd_buf[:, n * 512:(n + 1) * 512], preferred_element_type=F32)
        for t in range(4):
            for i in range(plane):
                mlp_out[i, 4 * n + t:4 * n + t + 1, :] = acc[i:i + 1, t * LANES:(t + 1) * LANES]

    def red_push(to_slot):
        return pltpu.make_async_remote_copy(
            src_ref=mlp_out.at[to_slot], dst_ref=mlp_in.at[my_slot], send_sem=red_send, recv_sem=red_recv,
            device_id={"seq": my_plane * plane + to_slot}, device_id_type=MESH)

    @pl.loop(1, plane)
    def _(d):
        red_push(lax.rem(my_slot + d, plane)).start()

    mlp_in[my_slot] = mlp_out[my_slot]
    others = mlp_in.at[pl.ds(0, plane - 1)]
    pltpu.make_async_copy(others, others, red_recv).wait()
    total = mlp_in[0]
    for i in range(1, plane):
        total = total + mlp_in[i]
    fin_out[...] = total
    fin = pltpu.make_async_remote_copy(
        src_ref=fin_out, dst_ref=fin_in, send_sem=fin_send, recv_sem=fin_recv,
        device_id={"model": 1 - core}, device_id_type=MESH)
    fin.start()
    fin.wait()
    out_ref[0:n_md, :] = (resid[0:n_md, :] + (fin_out[...] + fin_in[...])).astype(BF16)

    pltpu.make_async_copy(q_all.at[pl.ds(0, seqs - 1)], q_all.at[pl.ds(0, seqs - 1)], q_send).wait()
    pltpu.make_async_copy(others_part(part_in, seqs), others_part(part_in, seqs), part_send).wait()
    pltpu.make_async_copy(gone, gone, h2_send).wait()
    pltpu.make_async_copy(others, others, red_send).wait()


def others_part(ref, seqs):
    return ref.at[pl.ds(0, seqs - 1)]


def plane_size(seq_devs):
    return 16 if seq_devs % 16 == 0 else 4


def solution(mesh):
    model_devs = mesh.shape["model"]
    seq_devs = mesh.shape["seq"]

    def device_step(hidden, k_cache, v_cache, sel_blocks, g_attn, g_mlp, w_q, w_o, w_gate, w_up, w_down):
        model_dim = hidden.shape[1]
        batch, tokens, kv_local, head_dim = k_cache.shape
        n_md = model_dim // LANES
        pad_md = -(-n_md // 16) * 16
        plane = plane_size(seq_devs)
        tiles_ffn = w_gate.shape[1] // LANES
        tiles_max = -(-tiles_ffn // plane)
        width = w_q.shape[1] // model_devs
        small = jnp.stack([hidden.reshape(n_md, LANES), g_attn.reshape(n_md, LANES), g_mlp.reshape(n_md, LANES)])
        small = jnp.pad(small, ((0, 0), (0, pad_md - n_md), (0, 0)))
        kv_rows = tokens * kv_local
        k_rows = k_cache.reshape(batch, kv_rows, head_dim)
        v_rows = v_cache.reshape(batch, kv_rows, head_dim)
        cfg = (seq_devs, plane, n_md, tiles_ffn, tiles_max)
        any_spec = pl.BlockSpec(memory_space=pl.ANY)
        vmem_spec = pl.BlockSpec(memory_space=pltpu.VMEM)
        dma = pltpu.SemaphoreType.DMA
        out = pl.pallas_call(
            functools.partial(decode_kernel, cfg),
            out_shape=jax.ShapeDtypeStruct((n_md, LANES), BF16),
            in_specs=[vmem_spec, vmem_spec] + [any_spec] * 7,
            out_specs=vmem_spec,
            scratch_shapes=[
                pltpu.VMEM((batch, kv_rows, LANES), BF16),
                pltpu.VMEM((batch, kv_rows, LANES), BF16),
                pltpu.VMEM((width // 256, model_dim, 256), BF16),
                pltpu.VMEM((model_dim // 512, width, 512), BF16),
                pltpu.VMEM((model_dim, tiles_max * LANES), BF16),
                pltpu.VMEM((model_dim, tiles_max * LANES), BF16),
                pltpu.VMEM((tiles_max * LANES, model_dim), BF16),
                pltpu.VMEM((2, batch, 4, LANES), F32),
                pltpu.VMEM((16, model_dim), BF16),
                pltpu.VMEM((16, width), BF16),
                pltpu.VMEM((batch, 16, LANES), BF16),
                pltpu.VMEM((batch, 16, LANES), F32),
                pltpu.VMEM((batch, 16, LANES), F32),
                pltpu.VMEM((seq_devs + 8, LANES), F32),
                pltpu.VMEM((pad_md, LANES), F32),
                pltpu.VMEM((pad_md, LANES), F32),
                pltpu.VMEM((plane, pad_md, LANES), BF16),
                pltpu.VMEM((plane, n_md, LANES), F32),
                pltpu.VMEM((plane, n_md, LANES), F32),
                pltpu.VMEM((n_md, LANES), F32),
                pltpu.VMEM((n_md, LANES), F32),
                dma((width // 256,)), dma((2, seq_devs // plane)), dma((model_dim // 512,)), dma((3,)),
                dma, dma((seq_devs // plane,)), dma, dma, dma, dma, dma, dma, dma, dma, dma, dma,
            ],
            compiler_params=pltpu.CompilerParams(
                collective_id=0, has_side_effects=True, vmem_limit_bytes=64 * 1024 * 1024 - 128 * 1024),
            name="decode_step",
        )(small, sel_blocks, k_rows, v_rows, w_q, w_o, w_gate, w_up, w_down)
        return out.reshape(1, model_dim)

    cache_spec = P("data", "seq", "model", None)
    in_specs = (P(("data", "seq"), None), cache_spec, cache_spec, P("data", None, None), P(None), P(None), P(None, None), P(None, None), P(None, "model"), P(None, "model"), P("model", None))
    return jax.shard_map(device_step, mesh=mesh, in_specs=in_specs, out_specs=P(("data", "seq"), None), check_vma=False)
```

time: 246 us -> 63.9 us (0.26)
  waiting for transfers between devices: 93.3 us -> 0 us
  matrix products: 90.7 us -> 0 us
  Pallas kernels: 0 us -> 58.6 us
  starting transfers between devices: 21.5 us -> 0 us
  local copies, waits for them, and re-layouts: 23.8 us -> 2.88 us
  blocking collectives: 11.2 us -> 0 us
    all_to_all x2 -> x0, waiting for transfers between devices: 93.3 us -> none  [the longest x1 50 us: device_step(): k_recv = lax.all_to_all(k_send, 'seq', 0, 0, tiled=True)]
    dot_general x7 -> x0, matrix products: 90.7 us -> none  [the longest x1 23.7 us: device_step(): jnp.dot(hidden_act, w_down, preferred_element_type=jnp.float32)]
    pallas_call x0 -> x1, Pallas kernels: none -> 58.6 us  [device_step(): pl.pallas_call(functools.partial(decode_kernel, cfg), out_shape=jax.Shape...]
    all_to_all x2 -> x0, starting transfers between devices: 21.5 us -> none  [the longest x1 12.2 us: device_step(): k_recv = lax.all_to_all(k_send, 'seq', 0, 0, tiled=True)]
    gather x4 -> x0, local copies, waits for them, and re-layouts: 11.8 us -> none  [solution(): cache_h[idx_h]]
    psum x2 -> x0, blocking collectives: 11.2 us -> none  [the longest x1 7.85 us: device_step(): lax.psum(jnp.dot(attn_out, wo_local, preferred_element_type=jnp.float32),...]
    unnamed x13 -> x2, local copies, waits for them, and re-layouts: 11.5 us -> 2.88 us
  transfers between devices with their start and end apart: 2 -> 0, of which waited for: 2 -> 0; matrix products, arithmetic and copies ran while one was open for 10% -> 0% of each run, Pallas kernels for 0% -> 0%
where the time goes in v1:
time: 63.9 us; the launch traced here: 63.6 us
  Pallas kernels  58.6 us (92%)
  local copies, waits for them, and re-layouts  2.88 us (5%)
  other arithmetic  2.08 us (3%)
    pallas_call x1, Pallas kernels, device_step(): pl.pallas_call(functools.partial(decode_kernel, cfg), out_shape=jax.Shape...  58.6 us
    unnamed x2, local copies, waits for them, and re-layouts  2.88 us
    another operation x1, other arithmetic, device_step(): jnp.stack([hidden.reshape(n_md, LANES), g_attn.reshape(n_md, LANES), g_ml...  1.32 us

profile of v1, /device:TPU:1, one launch (start us, length us, event | category | flops | bytes accessed | tf_op | source)
XLA Modules:
  0.0 63.6 jit_solution(1392018645783374707)
XLA Ops:
  0.0 0.8 %reduce = bf16[3584]{0:T(1024)(128)(2,1)S(1)} reduce(bf16[1,3584]{1,0:T(2,128)(2,1)} %param.11, bf16[]{:T(256)} %constant.6), dimensions={0}, to_apply=%param.11.reduce_sub_computation | reduce | bytes 14338 | tf_op args[0]
  0.8 1.3 %fusion.4.small_ref = bf16[3,32,128]{2,1,0:T(8,128)(2,1)} fusion(bf16[1,28,128]{2,1,0:T(8,128)(2,1)} %bitcast.14, bf16[1,28,128]{2,1,0:T(8,128)(2,1)} %bitcast.15, bf16[1,28,128]{2,1,0:T(8,128)(2,1)S(1)} %bitcast.13), kind=kLoop, calls=%fused_computation.5 | loop fusion | flops 122880 | bytes 46080 | tf_op jit(solution)/shard_map/stack | solution.py:307
  2.1 1.6 %copy.12.sel_ref = s32[64,4,32]{2,1,0:T(4,128)} copy(s32[64,4,32]{0,2,1:T(8,128)} %param.14) | data formatting | bytes 65536 | tf_op args[3]
  3.7 58.6 %decode_step.1 = bf16[28,128]{1,0:T(8,128)(2,1)} custom-call(bf16[3,32,128]{2,1,0:T(8,128)(2,1)} %fusion.4.small_ref, s32[64,4,32]{2,1,0:T(4,128)} %copy.12.sel_ref, bf16[64,256,128]{2,1,0:T(8,128)(2,1)} %bitcast.10, bf16[64,256,128]{2,1,0:T(8,128)(2,1)} %bitcast.11, bf16[3584,3584]{1,0:T(8,128)(2,1)} %wq_hbm.1, bf16[3584,3584]{1,0:T(8,128)(2,1)} %wo_hbm.1, ...), custom_call_target="tpu_custom_call" | custom-call | tf_op jit(solution)/shard_map/decode_step/pallas_call | solution.py:316
  62.3 1.3 %copy.15 = bf16[1,1,28,128]{3,1,2,0:T(2,128)(2,1)} copy(bf16[1,1,28,128]{3,2,1,0:T(8,128)(2,1)} %bitcast.12) | data formatting | bytes 14336

commit v2 on v0

v2 whole, which is shorter than its diff:
```python
import functools

import jax
import jax.numpy as jnp
from jax import lax
from jax.experimental import pallas as pl
from jax.experimental.pallas import tpu as pltpu
from jax.sharding import PartitionSpec as P

MESH = pl.DeviceIdType.MESH
BLOCK_LEN = 64
NORM_EPS = 1e-5
LANES = 128
NEG_INF = float("-inf")
F32 = jnp.float32
BF16 = jnp.bfloat16


def row_iota(shape):
    return lax.broadcasted_iota(jnp.int32, shape, 0)


def torus_dims(seq_devs):
    side = round(seq_devs ** (1 / 3))
    return (side, side, side)


def mlp_box(dims):
    return (dims[0], 2, 2) if dims[0] > 2 else (2, 2, 1)


def offset_groups(dims):
    offsets = [(a, b, c) for a in range(dims[0]) for b in range(dims[1]) for c in range(dims[2])]

    def hops(o):
        return sum(min(d, n - d) for d, n in zip(o, dims))

    top = sum(n // 2 for n in dims)
    if top >= 6:
        bands = [(0, 1, 2), (3,), (6, 5), (4,)]
        push_bands = [(0, 1, 2), (6, 5), (4,), (3,)]
    else:
        bands = push_bands = [(0, 1), (2,), (3,)]
    pick = [[o for h in band for o in offsets if hops(o) == h] for band in bands]
    push = [o for band in push_bands for h in band for o in offsets if hops(o) == h]
    return push, pick


def decode_kernel(
    cfg,
    hid_hbm, ga_hbm, gm_hbm, sel_hbm, k_hbm, v_hbm, wq_hbm, wo_hbm, wg_hbm, wu_hbm, wd_hbm,
    out_ref,
    k_buf, v_buf, wq_buf, wo_buf, wg_buf, wu_buf, wd_buf,
    hid_ref, ga_ref, gm_ref, sel_ref, hit_buf, lhs_buf, olhs_buf,
    q_out, q_all, s_buf, p_buf, part_out, part_in, stat_buf,
    pair_out, pair_in, h2_all, mlp_out, mlp_in, fin_out, fin_in,
    small_sem, wq_sem, kv_sem, wo_sem, mlp_sem,
    q_send, q_recv, part_send, part_recv, pair_send, pair_recv, h2_send, h2_recv,
    red_send, red_recv, fin_send, fin_recv,
):
    seqs, n_md, tiles_ffn, tiles_max = cfg
    dims = torus_dims(seqs)
    box = mlp_box(dims)
    members = box[0] * box[1] * box[2]
    push_order, groups = offset_groups(dims)
    core = lax.axis_index("model")
    other = 1 - core
    me = lax.axis_index("seq")
    place = (me // (dims[1] * dims[2]), (me // dims[2]) % dims[1], me % dims[2])

    def seq_at(offset):
        z, y, x = (lax.rem(p + o, n) if o else p for p, o, n in zip(place, offset, dims))
        return (z * dims[1] + y) * dims[2] + x

    inner = tuple(p % n for p, n in zip(place, box))
    my_slot = (inner[0] * box[1] + inner[1]) * box[2] + inner[2]

    def member_at(offset):
        z, y, x = (lax.rem(p + o, n) if o else p for p, o, n in zip(inner, offset, box))
        slot = (z * box[1] + y) * box[2] + x
        whole = [p - i + v for p, i, v in zip(place, inner, (z, y, x))]
        return slot, (whole[0] * dims[1] + whole[1]) * dims[2] + whole[2]

    def box_hops(o):
        return sum(min(d, n - d) for d, n in zip(o, box))

    box_offsets = [(a, b, c) for a in range(box[0]) for b in range(box[1]) for c in range(box[2])]
    box_far_first = sorted(box_offsets, key=lambda o: (-box_hops(o), o))

    heads = 14
    width = heads * LANES
    q_chunks = -(-wq_buf.shape[1] // 512)
    o_chunks = wo_buf.shape[0]
    model_dim = n_md * LANES
    pad_md = pair_out.shape[0]
    k_parts = 4
    part_rows = model_dim // k_parts

    wq_cols = [(c, min(512, width - c)) for c in range(0, width, 512)]

    def wq_start(n):
        at, size = wq_cols[n]
        cols = pl.ds(pl.multiple_of(other * width + at, LANES), size)
        for part in range(k_parts):
            rows = pl.ds(part * part_rows, part_rows)
            pltpu.make_async_copy(wq_hbm.at[rows, cols], wq_buf.at[rows, pl.ds(at, size)], wq_sem.at[n]).start()

    def wq_wait(n):
        at, size = wq_cols[n]
        done = wq_buf.at[:, pl.ds(at, size)]
        pltpu.make_async_copy(done, done, wq_sem.at[n]).wait()

    kv_parts = 4
    kv_rows = seqs // kv_parts

    def kv_start(which):
        src, dst = ((k_hbm, k_buf), (v_hbm, v_buf))[which]
        for part in range(kv_parts):
            rows = pl.ds(part * kv_rows, kv_rows)
            pltpu.make_async_copy(src.at[rows], dst.at[rows], kv_sem.at[which]).start()

    def kv_wait(which):
        dst = (k_buf, v_buf)[which]
        pltpu.make_async_copy(dst, dst, kv_sem.at[which]).wait()

    def wo_copy(n):
        rows = pl.ds(pl.multiple_of(other * width, LANES), width)
        return pltpu.make_async_copy(wo_hbm.at[rows, pl.ds(n * 512, 512)], wo_buf.at[n], wo_sem.at[n])

    first_tile = (tiles_ffn * my_slot) // members
    my_tiles = (tiles_ffn * (my_slot + 1)) // members - first_tile
    ffn_cols = pl.ds(pl.multiple_of(first_tile * LANES, LANES), tiles_max * LANES)

    def up_start(which):
        src, dst = ((wg_hbm, wg_buf), (wu_hbm, wu_buf))[which]
        for part in range(k_parts):
            rows = pl.ds(part * part_rows, part_rows)
            pltpu.make_async_copy(src.at[rows, ffn_cols], dst.at[rows], mlp_sem.at[which]).start()

    def up_wait(which):
        dst = (wg_buf, wu_buf)[which]
        pltpu.make_async_copy(dst, dst, mlp_sem.at[which]).wait()

    wd_copy = pltpu.make_async_copy(wd_hbm.at[ffn_cols, :], wd_buf, mlp_sem.at[2])

    smalls = [
        pltpu.make_async_copy(src, dst, small_sem.at[n])
        for n, (src, dst) in enumerate(((hid_hbm, hid_ref), (ga_hbm, ga_ref), (gm_hbm, gm_ref), (sel_hbm, sel_ref)))
    ]
    for copy in smalls[:2]:
        copy.start()

    barrier = pltpu.get_barrier_semaphore()

    def greet(d):
        pl.semaphore_signal(barrier, inc=1, device_id={"model": other, "seq": lax.rem(me + d, seqs)}, device_id_type=MESH)

    early = seqs // 4
    pl.loop(0, early)(greet)
    for n in range(q_chunks):
        wq_start(n)
    for copy in smalls[2:]:
        copy.start()
    pl.loop(early, seqs)(greet)

    smalls[0].wait()
    smalls[1].wait()
    rows8 = row_iota((8, LANES))
    rows16 = row_iota((16, LANES))
    lane16 = lax.broadcasted_iota(jnp.int32, (16, LANES), 1)
    hid_parts = [jnp.zeros((8, LANES), F32) for _ in range(pad_md // 8)]
    for n in range(n_md):
        piece = jnp.broadcast_to(hid_ref[:, n * LANES:(n + 1) * LANES].astype(F32), (8, LANES))
        hid_parts[n // 8] = jnp.where(rows8 == n % 8, piece, hid_parts[n // 8])
    hid = jnp.concatenate(hid_parts, axis=0)
    fill = jnp.zeros((pad_md - n_md, LANES), F32)

    def norm(x, gain_ref):
        inv = lax.rsqrt(jnp.sum(x * x, keepdims=True) / model_dim + NORM_EPS)
        return (x * inv * jnp.concatenate([gain_ref[...].astype(F32), fill], axis=0)).astype(BF16)

    h_attn = norm(hid, ga_ref).astype(F32)
    for n in range(n_md):
        lhs_buf[:, n * LANES:(n + 1) * LANES] = jnp.broadcast_to(h_attn[n:n + 1, :], (16, LANES)).astype(BF16)

    q_tile = jnp.zeros((16, LANES), F32)
    head = 0
    for n in range(q_chunks):
        wq_wait(n)
        if n == q_chunks - 3:
            kv_start(0)
        if n == q_chunks - 2:
            kv_start(1)
        at, size = wq_cols[n]
        acc = jnp.dot(lhs_buf[...], wq_buf[:, at:at + size], preferred_element_type=F32) * (LANES ** -0.5)
        for t in range(size // LANES):
            q_tile = jnp.where(rows16 == head + head // 7, acc[:, t * LANES:(t + 1) * LANES], q_tile)
            head += 1
    q_out[...] = q_tile.astype(BF16)

    pl.semaphore_wait(barrier, seqs)

    def group_of(offset):
        back = tuple((n - o) % n for o, n in zip(offset, dims))
        return [k for k, group in enumerate(groups) if back in group][0]

    for offset in push_order:
        pltpu.make_async_remote_copy(
            src_ref=q_out, dst_ref=q_all.at[me], send_sem=q_send, recv_sem=q_recv.at[group_of(offset)],
            device_id={"model": other, "seq": seq_at(offset)}, device_id_type=MESH).start()
    for n in range(o_chunks):
        wo_copy(n).start()
    up_start(0)
    up_start(1)
    wd_copy.start()

    stat_buf[...] = jnp.zeros((LANES, LANES), F32)
    smalls[3].wait()
    for j in range(2):
        found = [
            jnp.max(jnp.where(sel_ref[g] == me * 2 + j, 1.0, 0.0), axis=0, keepdims=True)
            for g in range(4)
        ]
        for g in range(2):
            mine = jnp.where(core == 0, found[g], found[2 + g])
            column = jnp.broadcast_to(mine, (8, seqs)).T[:, 0:1]
            hit_buf[j, g] = jnp.broadcast_to(jnp.where(column > 0.5, 0.0, NEG_INF), (seqs, LANES))

    parity = ((lane16 % 2) == jnp.where(rows16 < 8, 0, 1)) & (rows16 % 8 != 7)
    order = [(k, i, seq_at(offset)) for k, group in enumerate(groups) for i, offset in enumerate(group)]
    tops = {}
    stats = {k: [jnp.zeros((16, LANES), F32)] * 2 for k in range(len(groups))}
    gap = 5
    slots = [None]
    for n, item in enumerate(order):
        if item[1] == 0 and item[0] == 1:
            slots += [None] * (3 * gap)
        slots.append((n,) + item)
    slots += [None] * (3 * gap)

    def spot(n):
        return slice(n * 16, (n + 1) * 16)

    def push_half(row, half):
        tile = pl.ds(half * 8, 8)
        pltpu.make_async_remote_copy(
            src_ref=part_out.at[row, tile], dst_ref=part_in.at[me, tile], send_sem=part_send, recv_sem=part_recv.at[half],
            device_id={"model": other, "seq": row}, device_id_type=MESH).start()

    def score_stage(n, k, i, row):
        if i == 0:
            arrived = q_all.at[pl.ds(0, len(groups[k]))]
            pltpu.make_async_copy(arrived, arrived, q_recv.at[k]).wait()
        if n == 0:
            kv_wait(0)
        scores = lax.dot_general(q_all[row], k_buf[row], (((1,), (1,)), ((), ())), preferred_element_type=F32)
        for j in range(2):
            hit_0 = jnp.broadcast_to(hit_buf[j, 0, pl.ds(row, 1), :], (16, LANES))
            hit_1 = jnp.broadcast_to(hit_buf[j, 1, pl.ds(row, 1), :], (16, LANES))
            bias = jnp.where(parity, jnp.where(rows16 < 8, hit_0, hit_1), NEG_INF)
            s_buf[spot(n), j * LANES:(j + 1) * LANES] = scores[:, j * LANES:(j + 1) * LANES] + bias

    def top_stage(n, k, i, row):
        tops[n] = jnp.max(s_buf[spot(n), :], axis=1, keepdims=True)

    def exp_stage(n, k, i, row):
        top = tops.pop(n)
        safe = jnp.where(top == NEG_INF, 0.0, top)
        exps = jnp.exp(s_buf[spot(n), :] - safe)
        p_buf[spot(n), :] = exps.astype(BF16)
        total = jnp.sum(exps, axis=1, keepdims=True)
        stats[k] = [jnp.where(lane16 == i, v, old) for v, old in zip((top, total), stats[k])]

    def value_stage(n, k, i, row):
        if n == 0:
            kv_wait(1)
        part_out[row] = jnp.dot(p_buf[spot(n), :], v_buf[row], preferred_element_type=F32)
        if i == len(groups[k]) - 1:
            stats_t = jnp.concatenate(stats[k], axis=0).T
            rows = [item[2] for item in order if item[0] == k]
            for m, to in enumerate(rows):
                part_out[to, 7:8, 0:32] = stats_t[m:m + 1, :]
                part_out[to, 15:16, 0:32] = stats_t[m:m + 1, :]
            for to in rows:
                push_half(to, 0)
            if k == 0:
                for to in rows:
                    push_half(to, 1)

    for t in range(len(slots)):
        for lag, stage in ((0, score_stage), (gap, top_stage), (2 * gap, exp_stage), (3 * gap, value_stage)):
            if t >= lag and slots[t - lag] is not None:
                stage(*slots[t - lag])
    for k in range(len(groups) - 1, 0, -1):
        for item in order:
            if item[0] == k:
                push_half(item[2], 1)

    proj = [jnp.zeros((8, LANES), F32) for _ in range(pad_md // 8)]
    half_width = width // 2
    for half in range(2):
        tile = slice(half * 8, half * 8 + 8)
        landed = part_in.at[:, pl.ds(half * 8, 8)]
        pltpu.make_async_copy(landed, landed, part_recv.at[half]).wait()
        for i in range(seqs):
            stat_buf[i:i + 1, :] = part_in[i, half * 8 + 7:half * 8 + 8, :]
        stat_t = stat_buf[...].T
        real = lax.broadcasted_iota(jnp.int32, (8, LANES), 1) < seqs
        top = jnp.where(real, stat_t[tile, :], NEG_INF)
        scale = jnp.exp(top - jnp.max(top, axis=1, keepdims=True))
        mass = jnp.where(real, stat_t[half * 8 + 16:half * 8 + 24, :], 0.0)
        denom = jnp.sum(scale * mass, axis=1, keepdims=True)
        sums = [jnp.zeros((8, LANES), F32) for _ in range(4)]
        for i in range(seqs):
            sums[i % 4] = sums[i % 4] + scale[:, i:i + 1] * part_in[i, tile, :]
        attn = (((sums[0] + sums[1]) + (sums[2] + sums[3])) / denom).astype(BF16).astype(F32)
        for r in range(7):
            olhs_buf[:, r * LANES:(r + 1) * LANES] = jnp.broadcast_to(attn[r:r + 1, :], (16, LANES)).astype(BF16)
        for n in range(o_chunks):
            if half == 0:
                wo_copy(n).wait()
            acc = jnp.dot(olhs_buf[...], wo_buf[n, half * half_width:(half + 1) * half_width, :], preferred_element_type=F32)
            for t in range(4):
                r = 4 * n + t
                here = jnp.where(rows8 == r % 8, acc[0:8, t * LANES:(t + 1) * LANES], 0.0)
                proj[r // 8] = proj[r // 8] + here
    for r in range(pad_md // 8):
        pair_out[r * 8:(r + 1) * 8, :] = proj[r]
    pair = pltpu.make_async_remote_copy(
        src_ref=pair_out, dst_ref=pair_in, send_sem=pair_send, recv_sem=pair_recv,
        device_id={"model": other}, device_id_type=MESH)
    pair.start()
    pair.wait()
    smalls[2].wait()
    resid = (hid + (pair_out[...] + pair_in[...])).astype(BF16).astype(F32)
    h2_all[my_slot] = norm(resid, gm_ref)

    for offset in box_far_first:
        if any(offset):
            pltpu.make_async_remote_copy(
                src_ref=h2_all.at[my_slot], dst_ref=h2_all.at[my_slot], send_sem=h2_send, recv_sem=h2_recv,
                device_id={"model": other, "seq": member_at(offset)[1]}, device_id_type=MESH).start()
    gone = h2_all.at[pl.ds(0, members - 1)]
    pltpu.make_async_copy(gone, gone, h2_recv).wait()
    rows = [h2_all[i].astype(F32) for i in range(members)]
    for n in range(n_md):
        tile = jnp.zeros((16, LANES), F32)
        for i in range(members):
            tile = jnp.where(rows16 == i, jnp.broadcast_to(rows[i][n:n + 1, :], (16, LANES)), tile)
        lhs_buf[:, n * LANES:(n + 1) * LANES] = tile.astype(BF16)

    up_wait(0)
    gate = jnp.dot(lhs_buf[...], wg_buf[...], preferred_element_type=F32).astype(BF16).astype(F32)
    up_wait(1)
    up = jnp.dot(lhs_buf[...], wu_buf[...], preferred_element_type=F32).astype(BF16).astype(F32)
    act = jax.nn.silu(gate) * up
    cols = lax.broadcasted_iota(jnp.int32, act.shape, 1)
    act = jnp.where(cols < my_tiles * LANES, act, 0.0).astype(BF16)
    wd_copy.wait()
    cut = min(16, n_md // 2 // 4 * 4) if n_md > 4 else 0
    pieces = [(0, cut), (cut, n_md)] if cut else [(0, n_md)]
    homes = [member_at(offset) for offset in box_far_first]
    for piece, (low, high) in enumerate(pieces):
        for n in range(low // 4, high // 4):
            acc = jnp.dot(act, wd_buf[:, n * 512:(n + 1) * 512], preferred_element_type=F32)
            for t in range(4):
                for i in range(members):
                    mlp_out[i, 4 * n + t:4 * n + t + 1, :] = acc[i:i + 1, t * LANES:(t + 1) * LANES]
        for slot, home in homes:
            tile = pl.ds(low, high - low)
            pltpu.make_async_remote_copy(
                src_ref=mlp_out.at[slot, tile], dst_ref=mlp_in.at[my_slot, tile], send_sem=red_send, recv_sem=red_recv.at[piece],
                device_id={"model": other, "seq": home}, device_id_type=MESH).start()

    finals = []
    for piece, (low, high) in enumerate(pieces):
        tile = pl.ds(low, high - low)
        landed = mlp_in.at[:, tile]
        pltpu.make_async_copy(landed, landed, red_recv.at[piece]).wait()
        total = mlp_in[0, low:high, :]
        for i in range(1, members):
            total = total + mlp_in[i, low:high, :]
        fin_out[low:high, :] = total
        fin = pltpu.make_async_remote_copy(
            src_ref=fin_out.at[tile], dst_ref=fin_in.at[tile], send_sem=fin_send.at[piece], recv_sem=fin_recv.at[piece],
            device_id={"model": other}, device_id_type=MESH)
        fin.start()
        finals.append(fin)
    for fin in finals:
        fin.wait()
    result = resid[0:n_md, :] + (fin_out[...] + fin_in[...])
    for n in range(n_md):
        out_ref[:, n * LANES:(n + 1) * LANES] = result[n:n + 1, :].astype(BF16)

    pltpu.make_async_copy(q_all, q_all, q_send).wait()
    pltpu.make_async_copy(part_in, part_in, part_send).wait()
    pltpu.make_async_copy(gone, gone, h2_send).wait()
    pltpu.make_async_copy(mlp_in, mlp_in, red_send).wait()


def solution(mesh):
    model_devs = mesh.shape["model"]
    seq_devs = mesh.shape["seq"]

    def device_step(hidden, k_cache, v_cache, sel_blocks, g_attn, g_mlp, w_q, w_o, w_gate, w_up, w_down):
        model_dim = hidden.shape[1]
        batch, tokens, kv_local, head_dim = k_cache.shape
        n_md = model_dim // LANES
        pad_md = -(-n_md // 16) * 16
        dims = torus_dims(seq_devs)
        box = mlp_box(dims)
        members = box[0] * box[1] * box[2]
        tiles_ffn = w_gate.shape[1] // LANES
        tiles_max = -(-tiles_ffn // members)
        width = w_q.shape[1] // model_devs
        kv_rows = tokens * kv_local
        k_rows = k_cache.reshape(batch, kv_rows, head_dim)
        v_rows = v_cache.reshape(batch, kv_rows, head_dim)
        cfg = (seq_devs, n_md, tiles_ffn, tiles_max)
        any_spec = pl.BlockSpec(memory_space=pl.ANY)
        vmem_spec = pl.BlockSpec(memory_space=pltpu.VMEM)
        dma = pltpu.SemaphoreType.DMA
        out = pl.pallas_call(
            functools.partial(decode_kernel, cfg),
            out_shape=jax.ShapeDtypeStruct((1, model_dim), BF16),
            in_specs=[any_spec] * 11,
            out_specs=vmem_spec,
            scratch_shapes=[
                pltpu.VMEM((batch, kv_rows, LANES), BF16),
                pltpu.VMEM((batch, kv_rows, LANES), BF16),
                pltpu.VMEM((model_dim, width), BF16),
                pltpu.VMEM((model_dim // 512, width, 512), BF16),
                pltpu.VMEM((model_dim, tiles_max * LANES), BF16),
                pltpu.VMEM((model_dim, tiles_max * LANES), BF16),
                pltpu.VMEM((tiles_max * LANES, model_dim), BF16),
                pltpu.VMEM((1, model_dim), BF16),
                pltpu.VMEM((n_md, LANES), BF16),
                pltpu.VMEM((n_md, LANES), BF16),
                pltpu.VMEM((4, sel_blocks.shape[2], batch), jnp.int32),
                pltpu.VMEM((2, 2, batch, LANES), F32),
                pltpu.VMEM((16, model_dim), BF16),
                pltpu.VMEM((16, width // 2), BF16),
                pltpu.VMEM((16, LANES), BF16),
                pltpu.VMEM((batch, 16, LANES), BF16),
                pltpu.VMEM((batch * 16, kv_rows), F32),
                pltpu.VMEM((batch * 16, kv_rows), BF16),
                pltpu.VMEM((batch, 16, LANES), F32),
                pltpu.VMEM((batch, 16, LANES), F32),
                pltpu.VMEM((LANES, LANES), F32),
                pltpu.VMEM((pad_md, LANES), F32),
                pltpu.VMEM((pad_md, LANES), F32),
                pltpu.VMEM((members, pad_md, LANES), BF16),
                pltpu.VMEM((members, n_md, LANES), F32),
                pltpu.VMEM((members, n_md, LANES), F32),
                pltpu.VMEM((n_md, LANES), F32),
                pltpu.VMEM((n_md, LANES), F32),
                dma((4,)), dma((-(-width // 512),)), dma((2,)), dma((model_dim // 512,)), dma((3,)),
                dma, dma((4,)), dma, dma((2,)), dma, dma, dma, dma, dma, dma((2,)), dma((2,)), dma((2,)),
            ],
            compiler_params=pltpu.CompilerParams(
                collective_id=0, has_side_effects=True, vmem_limit_bytes=54 * 1024 * 1024),
            name="decode_step",
        )(hidden, g_attn.reshape(n_md, LANES), g_mlp.reshape(n_md, LANES), sel_blocks.transpose(1, 2, 0), k_rows, v_rows, w_q, w_o, w_gate, w_up, w_down)
        return out

    cache_spec = P("data", "seq", "model", None)
    in_specs = (P(("data", "seq"), None), cache_spec, cache_spec, P("data", None, None), P(None), P(None), P(None, None), P(None, None), P(None, "model"), P(None, "model"), P("model", None))
    return jax.shard_map(device_step, mesh=mesh, in_specs=in_specs, out_specs=P(("data", "seq"), None), check_vma=False)
```

time: 246 us -> 45.3 us (0.18)
  waiting for transfers between devices: 93.3 us -> 0 us
  matrix products: 90.7 us -> 0 us
  Pallas kernels: 0 us -> 43.8 us
  local copies, waits for them, and re-layouts: 23.8 us -> 1.33 us
  starting transfers between devices: 21.5 us -> 0 us
  blocking collectives: 11.2 us -> 0 us
  other arithmetic: 3.1 us -> 0 us
    all_to_all x2 -> x0, waiting for transfers between devices: 93.3 us -> none  [the longest x1 50 us: device_step(): k_recv = lax.all_to_all(k_send, 'seq', 0, 0, tiled=True)]
    dot_general x7 -> x0, matrix products: 90.7 us -> none  [the longest x1 23.7 us: device_step(): jnp.dot(hidden_act, w_down, preferred_element_type=jnp.float32)]
    pallas_call x0 -> x1, Pallas kernels: none -> 43.8 us  [device_step(): pl.pallas_call(functools.partial(decode_kernel, cfg), out_shape=jax.Shape...]
    all_to_all x2 -> x0, starting transfers between devices: 21.5 us -> none  [the longest x1 12.2 us: device_step(): k_recv = lax.all_to_all(k_send, 'seq', 0, 0, tiled=True)]
    gather x4 -> x0, local copies, waits for them, and re-layouts: 11.8 us -> none  [solution(): cache_h[idx_h]]
    psum x2 -> x0, blocking collectives: 11.2 us -> none  [the longest x1 7.85 us: device_step(): lax.psum(jnp.dot(attn_out, wo_local, preferred_element_type=jnp.float32),...]
    unnamed x13 -> x1, local copies, waits for them, and re-layouts: 11.5 us -> 1.33 us
  transfers between devices with their start and end apart: 2 -> 0, of which waited for: 2 -> 0; matrix products, arithmetic and copies ran while one was open for 10% -> 0% of each run, Pallas kernels for 0% -> 0%
where the time goes in v2:
time: 45.3 us; the launch traced here: 45.1 us
  Pallas kernels  43.8 us (97%)
  local copies, waits for them, and re-layouts  1.33 us (3%)
    pallas_call x1, Pallas kernels, device_step(): pl.pallas_call(functools.partial(decode_kernel, cfg), out_shape=jax.Shape...  43.8 us
    unnamed x1, local copies, waits for them, and re-layouts  1.33 us

profile of v2, /device:TPU:1, one launch (start us, length us, event | category | flops | bytes accessed | tf_op | source)
XLA Modules:
  0.0 45.1 jit_solution(7540432435614729714)
XLA Ops:
  0.0 43.8 %decode_step.1 = bf16[1,3584]{1,0:T(2,128)(2,1)} custom-call(bf16[1,3584]{1,0:T(2,128)(2,1)} %hid_hbm.1, bf16[28,128]{1,0:T(8,128)(2,1)} %bitcast.8, bf16[28,128]{1,0:T(8,128)(2,1)} %bitcast.9, s32[4,32,64]{2,1,0:T(8,128)} %bitcast.7, bf16[64,256,128]{2,1,0:T(8,128)(2,1)} %bitcast.5, bf16[64,256,128]{2,1,0:T(8,128)(2,1)} %bitcast.6, ...), custom_call_target="tpu_custom_call" | custom-call | tf_op jit(solution)/shard_map/decode_step/pallas_call | solution.py:423
  43.8 1.3 %copy.13 = bf16[1,3584]{1,0:T(2,128)(2,1)} copy(bf16[1,3584]{1,0:T(2,128)(2,1)} %decode_step.1) | data formatting | bytes 14336

commit v3 on v2

--- a/solution.py
+++ b/solution.py
@@ -26,24 +26,23 @@
 
 
 def mlp_box(dims):
-    return (dims[0], 2, 2) if dims[0] > 2 else (2, 2, 1)
-
-
-def offset_groups(dims):
+    return (2, 2, dims[2]) if dims[2] > 2 else (1, 2, 2)
+
+
+def box_rows(dims):
+    box = mlp_box(dims)
+    spans = [range(0, n, m) for n, m in zip(dims, box)]
+    rows = []
+    for corner in [(z, y, x) for z in spans[0] for y in spans[1] for x in spans[2]]:
+        places = [(a, b, c) for a in range(box[0]) for b in range(box[1]) for c in range(box[2])]
+        cells = [[p + q for p, q in zip(corner, place)] for place in places]
+        rows.append([(z * dims[1] + y) * dims[2] + x for z, y, x in cells])
+    return rows
+
+
+def push_offsets(dims):
     offsets = [(a, b, c) for a in range(dims[0]) for b in range(dims[1]) for c in range(dims[2])]
-
-    def hops(o):
-        return sum(min(d, n - d) for d, n in zip(o, dims))
-
-    top = sum(n // 2 for n in dims)
-    if top >= 6:
-        bands = [(0, 1, 2), (3,), (6, 5), (4,)]
-        push_bands = [(0, 1, 2), (6, 5), (4,), (3,)]
-    else:
-        bands = push_bands = [(0, 1), (2,), (3,)]
-    pick = [[o for h in band for o in offsets if hops(o) == h] for band in bands]
-    push = [o for band in push_bands for h in band for o in offsets if hops(o) == h]
-    return push, pick
+    return sorted(offsets, key=lambda o: (-sum(min(d, n - d) for d, n in zip(o, dims)), o))
 
 
 def decode_kernel(
@@ -62,7 +61,7 @@
     dims = torus_dims(seqs)
     box = mlp_box(dims)
     members = box[0] * box[1] * box[2]
-    push_order, groups = offset_groups(dims)
+    push_order, groups = push_offsets(dims), box_rows(dims)
     core = lax.axis_index("model")
     other = 1 - core
     me = lax.axis_index("seq")
@@ -83,6 +82,15 @@
 
     def box_hops(o):
         return sum(min(d, n - d) for d, n in zip(o, box))
+
+    my_box = place[0] // box[0]
+    for p, n, m in zip(place[1:], dims[1:], box[1:]):
+        my_box = my_box * (n // m) + p // m
+
+    def row_in_box(k, j):
+        first = groups[k][0]
+        z, y, x = j // (box[1] * box[2]), (j // box[2]) % box[1], j % box[2]
+        return first + (z * dims[1] + y) * dims[2] + x
 
     box_offsets = [(a, b, c) for a in range(box[0]) for b in range(box[1]) for c in range(box[2])]
     box_far_first = sorted(box_offsets, key=lambda o: (-box_hops(o), o))
@@ -110,18 +118,24 @@
         done = wq_buf.at[:, pl.ds(at, size)]
         pltpu.make_async_copy(done, done, wq_sem.at[n]).wait()
 
-    kv_parts = 4
-    kv_rows = seqs // kv_parts
-
-    def kv_start(which):
+    runs = []
+    for k, rows in enumerate(groups):
+        for row in rows:
+            if runs and runs[-1][0] == k and runs[-1][1] + runs[-1][2] == row:
+                runs[-1][2] += 1
+            else:
+                runs.append([k, row, 1])
+
+    def kv_start(which, group):
         src, dst = ((k_hbm, k_buf), (v_hbm, v_buf))[which]
-        for part in range(kv_parts):
-            rows = pl.ds(part * kv_rows, kv_rows)
-            pltpu.make_async_copy(src.at[rows], dst.at[rows], kv_sem.at[which]).start()
-
-    def kv_wait(which):
-        dst = (k_buf, v_buf)[which]
-        pltpu.make_async_copy(dst, dst, kv_sem.at[which]).wait()
+        for k, row, count in runs:
+            if k == group:
+                rows = pl.ds(row, count)
+                pltpu.make_async_copy(src.at[rows], dst.at[rows], kv_sem.at[which, k]).start()
+
+    def kv_wait(which, k):
+        done = (k_buf, v_buf)[which].at[pl.ds(0, len(groups[k]))]
+        pltpu.make_async_copy(done, done, kv_sem.at[which, k]).wait()
 
     def wo_copy(n):
         rows = pl.ds(pl.multiple_of(other * width, LANES), width)
@@ -153,7 +167,7 @@
     barrier = pltpu.get_barrier_semaphore()
 
     def greet(d):
-        pl.semaphore_signal(barrier, inc=1, device_id={"model": other, "seq": lax.rem(me + d, seqs)}, device_id_type=MESH)
+        pl.semaphore_signal(barrier, inc=1, device_id={"model": other, "seq": d}, device_id_type=MESH)
 
     early = seqs // 4
     pl.loop(0, early)(greet)
@@ -187,26 +201,27 @@
     head = 0
     for n in range(q_chunks):
         wq_wait(n)
-        if n == q_chunks - 3:
-            kv_start(0)
         if n == q_chunks - 2:
-            kv_start(1)
+            kv_start(0, 0)
+            kv_start(1, 0)
+        if n == q_chunks - 1:
+            for k in range(1, len(groups)):
+                kv_start(0, k)
+                kv_start(1, k)
         at, size = wq_cols[n]
-        acc = jnp.dot(lhs_buf[...], wq_buf[:, at:at + size], preferred_element_type=F32) * (LANES ** -0.5)
-        for t in range(size // LANES):
-            q_tile = jnp.where(rows16 == head + head // 7, acc[:, t * LANES:(t + 1) * LANES], q_tile)
-            head += 1
+        span = 512 if size == 512 else LANES
+        for low in range(at, at + size, span):
+            acc = jnp.dot(lhs_buf[...], wq_buf[:, low:low + span], preferred_element_type=F32) * (LANES ** -0.5)
+            for t in range(span // LANES):
+                q_tile = jnp.where(rows16 == head + head // 7, acc[:, t * LANES:(t + 1) * LANES], q_tile)
+                head += 1
     q_out[...] = q_tile.astype(BF16)
 
     pl.semaphore_wait(barrier, seqs)
-
-    def group_of(offset):
-        back = tuple((n - o) % n for o, n in zip(offset, dims))
-        return [k for k, group in enumerate(groups) if back in group][0]
 
     for offset in push_order:
         pltpu.make_async_remote_copy(
-            src_ref=q_out, dst_ref=q_all.at[me], send_sem=q_send, recv_sem=q_recv.at[group_of(offset)],
+            src_ref=q_out, dst_ref=q_all.at[me], send_sem=q_send, recv_sem=q_recv.at[my_box],
             device_id={"model": other, "seq": seq_at(offset)}, device_id_type=MESH).start()
     for n in range(o_chunks):
         wo_copy(n).start()
@@ -227,13 +242,14 @@
             hit_buf[j, g] = jnp.broadcast_to(jnp.where(column > 0.5, 0.0, NEG_INF), (seqs, LANES))
 
     parity = ((lane16 % 2) == jnp.where(rows16 < 8, 0, 1)) & (rows16 % 8 != 7)
-    order = [(k, i, seq_at(offset)) for k, group in enumerate(groups) for i, offset in enumerate(group)]
+    order = [(k, i, row) for k, group in enumerate(groups) for i, row in enumerate(group)]
     tops = {}
     stats = {k: [jnp.zeros((16, LANES), F32)] * 2 for k in range(len(groups))}
     gap = 5
+    drains = ()
     slots = [None]
     for n, item in enumerate(order):
-        if item[1] == 0 and item[0] == 1:
+        if item[1] == 0 and item[0] in drains:
             slots += [None] * (3 * gap)
         slots.append((n,) + item)
     slots += [None] * (3 * gap)
@@ -247,16 +263,20 @@
             src_ref=part_out.at[row, tile], dst_ref=part_in.at[me, tile], send_sem=part_send, recv_sem=part_recv.at[half],
             device_id={"model": other, "seq": row}, device_id_type=MESH).start()
 
+    def push_box(k, half):
+        for i in range(members):
+            push_half(row_in_box(k, lax.rem(my_slot + i, members)), half)
+
     def score_stage(n, k, i, row):
         if i == 0:
             arrived = q_all.at[pl.ds(0, len(groups[k]))]
             pltpu.make_async_copy(arrived, arrived, q_recv.at[k]).wait()
-        if n == 0:
-            kv_wait(0)
+            kv_wait(0, k)
+            kv_wait(1, k)
         scores = lax.dot_general(q_all[row], k_buf[row], (((1,), (1,)), ((), ())), preferred_element_type=F32)
         for j in range(2):
-            hit_0 = jnp.broadcast_to(hit_buf[j, 0, pl.ds(row, 1), :], (16, LANES))
-            hit_1 = jnp.broadcast_to(hit_buf[j, 1, pl.ds(row, 1), :], (16, LANES))
+            hit_0 = jnp.broadcast_to(hit_buf[j, 0, row:row + 1, :], (16, LANES))
+            hit_1 = jnp.broadcast_to(hit_buf[j, 1, row:row + 1, :], (16, LANES))
             bias = jnp.where(parity, jnp.where(rows16 < 8, hit_0, hit_1), NEG_INF)
             s_buf[spot(n), j * LANES:(j + 1) * LANES] = scores[:, j * LANES:(j + 1) * LANES] + bias
 
@@ -272,8 +292,6 @@
         stats[k] = [jnp.where(lane16 == i, v, old) for v, old in zip((top, total), stats[k])]
 
     def value_stage(n, k, i, row):
-        if n == 0:
-            kv_wait(1)
         part_out[row] = jnp.dot(p_buf[spot(n), :], v_buf[row], preferred_element_type=F32)
         if i == len(groups[k]) - 1:
             stats_t = jnp.concatenate(stats[k], axis=0).T
@@ -281,20 +299,15 @@
             for m, to in enumerate(rows):
                 part_out[to, 7:8, 0:32] = stats_t[m:m + 1, :]
                 part_out[to, 15:16, 0:32] = stats_t[m:m + 1, :]
-            for to in rows:
-                push_half(to, 0)
-            if k == 0:
-                for to in rows:
-                    push_half(to, 1)
+            push_box(k, 0)
+            if k > 0:
+                push_box(k - 1, 1)
 
     for t in range(len(slots)):
         for lag, stage in ((0, score_stage), (gap, top_stage), (2 * gap, exp_stage), (3 * gap, value_stage)):
             if t >= lag and slots[t - lag] is not None:
                 stage(*slots[t - lag])
-    for k in range(len(groups) - 1, 0, -1):
-        for item in order:
-            if item[0] == k:
-                push_half(item[2], 1)
+    push_box(len(groups) - 1, 1)
 
     proj = [jnp.zeros((8, LANES), F32) for _ in range(pad_md // 8)]
     half_width = width // 2
@@ -302,23 +315,26 @@
         tile = slice(half * 8, half * 8 + 8)
         landed = part_in.at[:, pl.ds(half * 8, 8)]
         pltpu.make_async_copy(landed, landed, part_recv.at[half]).wait()
-        for i in range(seqs):
-            stat_buf[i:i + 1, :] = part_in[i, half * 8 + 7:half * 8 + 8, :]
-        stat_t = stat_buf[...].T
-        real = lax.broadcasted_iota(jnp.int32, (8, LANES), 1) < seqs
-        top = jnp.where(real, stat_t[tile, :], NEG_INF)
-        scale = jnp.exp(top - jnp.max(top, axis=1, keepdims=True))
-        mass = jnp.where(real, stat_t[half * 8 + 16:half * 8 + 24, :], 0.0)
-        denom = jnp.sum(scale * mass, axis=1, keepdims=True)
+        if half == 0:
+            for i in range(seqs):
+                stat_buf[i:i + 1, :] = part_in[i, 7:8, :]
+            stat_t = stat_buf[...].T
+            real = lax.broadcasted_iota(jnp.int32, (16, LANES), 1) < seqs
+            top = jnp.where(real, stat_t[0:16, :], NEG_INF)
+            scales = jnp.exp(top - jnp.max(top, axis=1, keepdims=True))
+            mass = jnp.where(real, stat_t[16:32, :], 0.0)
+            denoms = jnp.sum(scales * mass, axis=1, keepdims=True)
+        scale, denom = scales[tile, :], denoms[tile, :]
         sums = [jnp.zeros((8, LANES), F32) for _ in range(4)]
         for i in range(seqs):
             sums[i % 4] = sums[i % 4] + scale[:, i:i + 1] * part_in[i, tile, :]
         attn = (((sums[0] + sums[1]) + (sums[2] + sums[3])) / denom).astype(BF16).astype(F32)
         for r in range(7):
             olhs_buf[:, r * LANES:(r + 1) * LANES] = jnp.broadcast_to(attn[r:r + 1, :], (16, LANES)).astype(BF16)
+        if half == 0:
+            for n in range(o_chunks):
+                wo_copy(n).wait()
         for n in range(o_chunks):
-            if half == 0:
-                wo_copy(n).wait()
             acc = jnp.dot(olhs_buf[...], wo_buf[n, half * half_width:(half + 1) * half_width, :], preferred_element_type=F32)
             for t in range(4):
                 r = 4 * n + t
@@ -350,19 +366,26 @@
         lhs_buf[:, n * LANES:(n + 1) * LANES] = tile.astype(BF16)
 
     up_wait(0)
+    up_wait(1)
+    wd_copy.wait()
     gate = jnp.dot(lhs_buf[...], wg_buf[...], preferred_element_type=F32).astype(BF16).astype(F32)
-    up_wait(1)
     up = jnp.dot(lhs_buf[...], wu_buf[...], preferred_element_type=F32).astype(BF16).astype(F32)
     act = jax.nn.silu(gate) * up
     cols = lax.broadcasted_iota(jnp.int32, act.shape, 1)
     act = jnp.where(cols < my_tiles * LANES, act, 0.0).astype(BF16)
-    wd_copy.wait()
     cut = min(16, n_md // 2 // 4 * 4) if n_md > 4 else 0
     pieces = [(0, cut), (cut, n_md)] if cut else [(0, n_md)]
     homes = [member_at(offset) for offset in box_far_first]
+
+    def down(n):
+        return jnp.dot(act, wd_buf[:, n * 512:(n + 1) * 512], preferred_element_type=F32)
+
+    ahead = down(0)
     for piece, (low, high) in enumerate(pieces):
         for n in range(low // 4, high // 4):
-            acc = jnp.dot(act, wd_buf[:, n * 512:(n + 1) * 512], preferred_element_type=F32)
+            acc = ahead
+            if n + 1 < o_chunks:
+                ahead = down(n + 1)
             for t in range(4):
                 for i in range(members):
                     mlp_out[i, 4 * n + t:4 * n + t + 1, :] = acc[i:i + 1, t * LANES:(t + 1) * LANES]
@@ -454,8 +477,8 @@
                 pltpu.VMEM((members, n_md, LANES), F32),
                 pltpu.VMEM((n_md, LANES), F32),
                 pltpu.VMEM((n_md, LANES), F32),
-                dma((4,)), dma((-(-width // 512),)), dma((2,)), dma((model_dim // 512,)), dma((3,)),
-                dma, dma((4,)), dma, dma((2,)), dma, dma, dma, dma, dma, dma((2,)), dma((2,)), dma((2,)),
+                dma((4,)), dma((-(-width // 512),)), dma((2, 5)), dma((model_dim // 512,)), dma((3,)),
+                dma, dma((5,)), dma, dma((2,)), dma, dma, dma, dma, dma, dma((2,)), dma((2,)), dma((2,)),
             ],
             compiler_params=pltpu.CompilerParams(
                 collective_id=0, has_side_effects=True, vmem_limit_bytes=54 * 1024 * 1024),

time: 45.3 us -> 41.7 us (0.921)
  Pallas kernels: 43.8 us -> 40.1 us
    pallas_call x1, Pallas kernels: 43.8 us -> 40.1 us  [device_step(): pl.pallas_call(functools.partial(decode_kernel, cfg), out_shape=jax.Shape...]
where the time goes in v3:
time: 41.7 us; the launch traced here: 41.5 us
  Pallas kernels  40.1 us (96%)
  local copies, waits for them, and re-layouts  1.33 us (3%)
    pallas_call x1, Pallas kernels, device_step(): pl.pallas_call(functools.partial(decode_kernel, cfg), out_shape=jax.Shape...  40.1 us
    unnamed x1, local copies, waits for them, and re-layouts  1.33 us

profile of v3, /device:TPU:1, one launch (start us, length us, event | category | flops | bytes accessed | tf_op | source)
XLA Modules:
  0.0 41.5 jit_solution(6399145828350921605)
XLA Ops:
  0.0 40.1 %decode_step.1 = bf16[1,3584]{1,0:T(2,128)(2,1)} custom-call(bf16[1,3584]{1,0:T(2,128)(2,1)} %hid_hbm.1, bf16[28,128]{1,0:T(8,128)(2,1)} %bitcast.8, bf16[28,128]{1,0:T(8,128)(2,1)} %bitcast.9, s32[4,32,64]{2,1,0:T(8,128)} %bitcast.7, bf16[64,256,128]{2,1,0:T(8,128)(2,1)} %bitcast.5, bf16[64,256,128]{2,1,0:T(8,128)(2,1)} %bitcast.6, ...), custom_call_target="tpu_custom_call" | custom-call | tf_op jit(solution)/shard_map/decode_step/pallas_call | solution.py:446
  40.2 1.3 %copy.13 = bf16[1,3584]{1,0:T(2,128)(2,1)} copy(bf16[1,3584]{1,0:T(2,128)(2,1)} %decode_step.1) | data formatting | bytes 14336

commit v4 on v3

--- a/solution.py
+++ b/solution.py
@@ -245,8 +245,8 @@
     order = [(k, i, row) for k, group in enumerate(groups) for i, row in enumerate(group)]
     tops = {}
     stats = {k: [jnp.zeros((16, LANES), F32)] * 2 for k in range(len(groups))}
-    gap = 5
-    drains = ()
+    gap = 4
+    drains = (1,)
     slots = [None]
     for n, item in enumerate(order):
         if item[1] == 0 and item[0] in drains:
@@ -300,7 +300,9 @@
                 part_out[to, 7:8, 0:32] = stats_t[m:m + 1, :]
                 part_out[to, 15:16, 0:32] = stats_t[m:m + 1, :]
             push_box(k, 0)
-            if k > 0:
+            if k == 0:
+                push_box(0, 1)
+            if k > 1:
                 push_box(k - 1, 1)
 
     for t in range(len(slots)):
@@ -373,8 +375,7 @@
     act = jax.nn.silu(gate) * up
     cols = lax.broadcasted_iota(jnp.int32, act.shape, 1)
     act = jnp.where(cols < my_tiles * LANES, act, 0.0).astype(BF16)
-    cut = min(16, n_md // 2 // 4 * 4) if n_md > 4 else 0
-    pieces = [(0, cut), (cut, n_md)] if cut else [(0, n_md)]
+    pieces = [(0, 8), (8, 16), (16, n_md)] if n_md > 16 else [(0, n_md)]
     homes = [member_at(offset) for offset in box_far_first]
 
     def down(n):
@@ -445,7 +446,7 @@
         dma = pltpu.SemaphoreType.DMA
         out = pl.pallas_call(
             functools.partial(decode_kernel, cfg),
-            out_shape=jax.ShapeDtypeStruct((1, model_dim), BF16),
+            out_shape=pltpu.VMEM((1, model_dim), BF16),
             in_specs=[any_spec] * 11,
             out_specs=vmem_spec,
             scratch_shapes=[
@@ -478,7 +479,7 @@
                 pltpu.VMEM((n_md, LANES), F32),
                 pltpu.VMEM((n_md, LANES), F32),
                 dma((4,)), dma((-(-width // 512),)), dma((2, 5)), dma((model_dim // 512,)), dma((3,)),
-                dma, dma((5,)), dma, dma((2,)), dma, dma, dma, dma, dma, dma((2,)), dma((2,)), dma((2,)),
+                dma, dma((5,)), dma, dma((2,)), dma, dma, dma, dma, dma, dma((3,)), dma((3,)), dma((3,)),
             ],
             compiler_params=pltpu.CompilerParams(
                 collective_id=0, has_side_effects=True, vmem_limit_bytes=54 * 1024 * 1024),

time: 41.7 us -> 39.8 us (0.954)
  Pallas kernels: 40.1 us -> 39 us
  local copies, waits for them, and re-layouts: 1.33 us -> 0.6 us
    pallas_call x1, Pallas kernels: 40.1 us -> 39 us  [device_step(): pl.pallas_call(functools.partial(decode_kernel, cfg), out_shape=pltpu.VME...]
    unnamed x1, local copies, waits for them, and re-layouts: 1.33 us -> 0.6 us
where the time goes in v4:
time: 39.8 us; the launch traced here: 39.6 us
  Pallas kernels  39 us (98%)
  local copies, waits for them, and re-layouts  0.6 us (2%)
    pallas_call x1, Pallas kernels, device_step(): pl.pallas_call(functools.partial(decode_kernel, cfg), out_shape=pltpu.VME...  39 us

profile of v4, /device:TPU:1, one launch (start us, length us, event | category | flops | bytes accessed | tf_op | source)
XLA Modules:
  0.0 39.6 jit_solution(18093195453437986331)
XLA Ops:
  0.0 39.0 %decode_step.1 = bf16[1,3584]{1,0:T(2,128)(2,1)S(1)} custom-call(bf16[1,3584]{1,0:T(2,128)(2,1)} %hid_hbm.1, bf16[28,128]{1,0:T(8,128)(2,1)} %bitcast.8, bf16[28,128]{1,0:T(8,128)(2,1)} %bitcast.9, s32[4,32,64]{2,1,0:T(8,128)} %bitcast.7, bf16[64,256,128]{2,1,0:T(8,128)(2,1)} %bitcast.5, bf16[64,256,128]{2,1,0:T(8,128)(2,1)} %bitcast.6, ...), custom_call_target="tpu_custom_call" | custom-call | tf_op jit(solution)/shard_map/decode_step/pallas_call | solution.py:447
  39.0 0.6 %copy.13 = bf16[1,3584]{1,0:T(2,128)(2,1)} copy(bf16[1,3584]{1,0:T(2,128)(2,1)S(1)} %decode_step.1) | data formatting | bytes 14336
